TPU v7x, 8 devices: a whole 2x2x1 slice. The times are simulated.
8 devices in a mesh: dp: 1 (over z), cfg: 2 (over y), tp: 4 (over x, core).
Axes of the slice: x: 2, y: 2, z: 1, core: 2. Of those that a mesh axis runs over, the one named last changes fastest.
Arguments:
- hidden: bfloat16 [2, 4096, 1152], P(('dp', 'cfg'))
- caption: bfloat16 [2, 120, 1152], P(('dp', 'cfg'))
- cap_len: int32 [2], P(('dp', 'cfg'))
- t_block: bfloat16 [1, 6912], P('dp')
- t_embed: bfloat16 [1, 1152], P('dp')
- x_t: float32 [1, 128, 128, 4], P('dp')
- alpha_bar: float32 [1, 2], P('dp')
- mod_table: bfloat16 [2, 6, 1152], replicated
- w_qkv: bfloat16 [2, 1152, 3, 16, 72], P(None, None, None, 'tp')
- w_proj: bfloat16 [2, 16, 72, 1152], P(None, 'tp')
- w_cq: bfloat16 [2, 1152, 16, 72], P(None, None, 'tp')
- w_ckv: bfloat16 [2, 1152, 2, 16, 72], P(None, None, None, 'tp')
- w_cproj: bfloat16 [2, 16, 72, 1152], P(None, 'tp')
- w_fc1: bfloat16 [2, 1152, 4608], P(None, None, 'tp')
- w_fc2: bfloat16 [2, 4608, 1152], P(None, 'tp')
- final_table: bfloat16 [2, 1152], replicated
- w_out: bfloat16 [1152, 32], replicated
- b_out: bfloat16 [32], replicated
Outputs:
- output: float32 [1, 128, 128, 4], P('dp')
All inputs are finite; a program needn't handle non-finite values.
Results may differ from a plain program's by a relative error of at most 0.0120919.
Values are sent between devices in bfloat16 or wider.
A program may use at most 1 GiB of HBM per device.

v0:
```python
import jax
import jax.numpy as jnp
from jax import lax
from jax.sharding import PartitionSpec as P

GUIDANCE = 4.5
LN_EPS = 1e-6


def layer_norm(values):
    mean_val = jnp.mean(values, axis=-1, keepdims=True)
    centered = values - mean_val
    variance = jnp.mean(centered * centered, axis=-1, keepdims=True)
    return centered * lax.rsqrt(variance + LN_EPS)


def attention(queries, key_vecs, values, key_mask):
    qk_scale = queries.shape[-1] ** -0.5
    scores = jnp.einsum('rqhd,rkhd->rhqk', queries, key_vecs, preferred_element_type=jnp.float32) * qk_scale
    if key_mask is not None:
        scores = jnp.where(key_mask, scores, -1e30)
    attn_prob = jax.nn.softmax(scores, axis=-1).astype(jnp.bfloat16)
    return jnp.einsum('rhqk,rkhd->rqhd', attn_prob, values, preferred_element_type=jnp.float32).astype(jnp.bfloat16)


def tp_block(residual, caption, key_mask, mod_rows, w_qkv, w_proj, w_cq, w_ckv, w_cproj, w_fc1, w_fc2):
    attn_in = (layer_norm(residual) * (1.0 + mod_rows[:, None, 1]) + mod_rows[:, None, 0]).astype(jnp.bfloat16)
    qkv_out = jnp.einsum('rnd,dshe->rnshe', attn_in, w_qkv, preferred_element_type=jnp.float32).astype(jnp.bfloat16)
    self_o = attention(qkv_out[:, :, 0], qkv_out[:, :, 1], qkv_out[:, :, 2], None)
    self_part = jnp.einsum('rnhe,hed->rnd', self_o, w_proj, preferred_element_type=jnp.float32).astype(jnp.bfloat16)
    residual = residual + mod_rows[:, None, 2] * lax.psum(self_part, 'tp').astype(jnp.float32)
    cross_q = jnp.einsum('rnd,dhe->rnhe', residual.astype(jnp.bfloat16), w_cq, preferred_element_type=jnp.float32).astype(jnp.bfloat16)
    cross_kv = jnp.einsum('rtd,dshe->rtshe', caption, w_ckv, preferred_element_type=jnp.float32).astype(jnp.bfloat16)
    cross_o = attention(cross_q, cross_kv[:, :, 0], cross_kv[:, :, 1], key_mask)
    cross_part = jnp.einsum('rnhe,hed->rnd', cross_o, w_cproj, preferred_element_type=jnp.float32).astype(jnp.bfloat16)
    residual = residual + lax.psum(cross_part, 'tp').astype(jnp.float32)
    mlp_in = (layer_norm(residual) * (1.0 + mod_rows[:, None, 4]) + mod_rows[:, None, 3]).astype(jnp.bfloat16)
    mlp_hidden = jax.nn.gelu(jnp.einsum('rnd,df->rnf', mlp_in, w_fc1, preferred_element_type=jnp.float32), approximate=True).astype(jnp.bfloat16)
    mlp_part = jnp.einsum('rnf,fd->rnd', mlp_hidden, w_fc2, preferred_element_type=jnp.float32).astype(jnp.bfloat16)
    return residual + mod_rows[:, None, 5] * lax.psum(mlp_part, 'tp').astype(jnp.float32)


def final_layer(residual, final_table, emb_rows, w_out, b_out, side_len):
    shift_scale = final_table.astype(jnp.float32)[None] + emb_rows[:, None]
    final_in = (layer_norm(residual) * (1.0 + shift_scale[:, None, 1]) + shift_scale[:, None, 0]).astype(jnp.bfloat16)
    out_tok = jnp.einsum('rnd,dc->rnc', final_in, w_out, preferred_element_type=jnp.float32) + b_out.astype(jnp.float32)
    n_rows = residual.shape[0]
    grid_side = side_len // 2
    patches = out_tok.reshape(n_rows, grid_side, grid_side, 2, 2, 8)[:, :, :, :, :, :4]
    return patches.transpose(0, 1, 3, 2, 4, 5).reshape(n_rows, side_len, side_len, 4)


def guidance_mix(eps_all):
    n_images = eps_all.shape[0] // 2
    eps_uncond = eps_all[n_images:]
    return eps_uncond + GUIDANCE * (eps_all[:n_images] - eps_uncond)


def ddim_update(guided, x_t, alpha_bar):
    abar_t = alpha_bar[:, 0][:, None, None, None]
    abar_prev = alpha_bar[:, 1][:, None, None, None]
    x_zero = (x_t - jnp.sqrt(1.0 - abar_t) * guided) / jnp.sqrt(abar_t)
    return jnp.sqrt(abar_prev) * x_zero + jnp.sqrt(1.0 - abar_prev) * guided


def solution(mesh):
    row_spec = P(('dp', 'cfg'))
    part_spec = P('dp')
    in_specs = (row_spec, row_spec, row_spec, part_spec, part_spec, part_spec, part_spec, P(),
                P(None, None, None, 'tp'), P(None, 'tp'), P(None, None, 'tp'), P(None, None, None, 'tp'),
                P(None, 'tp'), P(None, None, 'tp'), P(None, 'tp'), P(), P(), P())

    def local_step(hidden, caption, cap_len, t_block, t_embed, x_t, alpha_bar, mod_table, w_qkv, w_proj, w_cq, w_ckv, w_cproj, w_fc1, w_fc2, final_table, w_out, b_out):
        n_rows = hidden.shape[0]
        model_dim = hidden.shape[2]
        row_start = (lax.axis_index('cfg') * n_rows) % t_block.shape[0]
        t_rows = lax.dynamic_slice_in_dim(t_block, row_start, n_rows, axis=0).astype(jnp.float32).reshape(n_rows, 6, model_dim)
        emb_rows = lax.dynamic_slice_in_dim(t_embed, row_start, n_rows, axis=0).astype(jnp.float32)
        key_mask = (jnp.arange(caption.shape[1])[None, :] < cap_len[:, None])[:, None, None, :]
        residual = hidden.astype(jnp.float32)
        for layer_idx in range(mod_table.shape[0]):
            mod_rows = mod_table[layer_idx].astype(jnp.float32)[None] + t_rows
            residual = tp_block(residual, caption, key_mask, mod_rows, w_qkv[layer_idx], w_proj[layer_idx], w_cq[layer_idx], w_ckv[layer_idx], w_cproj[layer_idx], w_fc1[layer_idx], w_fc2[layer_idx])
        eps_local = final_layer(residual, final_table, emb_rows, w_out, b_out, x_t.shape[1])
        eps_all = lax.all_gather(eps_local, 'cfg', axis=0, tiled=True)
        return ddim_update(guidance_mix(eps_all), x_t, alpha_bar)

    return jax.shard_map(local_step, mesh=mesh, in_specs=in_specs, out_specs=part_spec, check_vma=False)
```

profile of v0, /device:TPU:0, one launch (start us, length us, event | category | flops | bytes accessed | tf_op | source)
XLA Modules:
  0.0 1755.0 jit_solution(14938342618310211981)
XLA Ops:
  20.3 15.8 fusion.73
  45.1 106.8 %fusion.215 = (f32[4,4096]{1,0:T(4,128)S(1)}, f32[4,4096,4096]{1,2,0:T(8,128)}) fusion(bf16[1,4096,3,4,72]{1,4,3,2,0:T(8,128)(2,1)} %convert_bitcast_fusion.1), kind=kOutput, calls=%fused_computation.246 | convolution fusion | flops 9865007104 | bytes 273219584 | tf_op jit(solution)/shard_map/sub | solution.py:22
  151.9 83.4 %fusion.256 = bf16[4096,4,72]{0,2,1:T(8,128)(2,1)} fusion(f32[4,4096,4096]{1,2,0:T(8,128)} %get-tuple-element.36, f32[4,4096]{1,0:T(4,128)S(1)} %get-tuple-element.35, bf16[1,4096,3,4,72]{1,4,3,2,0:T(8,128)(2,1)} %convert_bitcast_fusion.1), kind=kOutput, calls=%bitcast_fusion.clone.2 | convolution fusion | flops 9799073792 | bytes 273219584 | tf_op jit(solution)/shard_map/rhqk,rkhd->rqhd/dot_general | solution.py:23
  251.1 161.1 %all-reduce.7.cloned.1.call-done = bf16[1,4096,1152]{2,1,0:T(8,128)(2,1)} async-done(((bf16[1,4096,1152]{2,1,0:T(8,128)(2,1)}), bf16[1,4096,1152]{2,1,0:T(8,128)(2,1)}) %all-reduce.7.cloned.1.call-update) | async-done | bytes 9437200 | tf_op jit(solution)/shard_map/psum | solution.py:31
  432.3 12.9 fusion.44
  445.3 164.4 %all-reduce.9.cloned.1.call-done = bf16[1,4096,1152]{2,1,0:T(8,128)(2,1)} async-done(((bf16[1,4096,1152]{2,1,0:T(8,128)(2,1)}), bf16[1,4096,1152]{2,1,0:T(8,128)(2,1)}) %all-reduce.9.cloned.1.call-update) | async-done | bytes 9437200 | tf_op jit(solution)/shard_map/psum | solution.py:36
  609.7 11.9 fusion.207
  621.6 10.2 multiply_reduce_fusion.5
  631.9 22.9 %fusion.31.clone.5 = bf16[4096,1152]{1,0:T(8,128)(2,1)} fusion(f32[1152]{0:T(1024)S(1)} %copy-done.21, f32[1152]{0:T(1024)S(1)} %copy-done.20, f32[4096]{0:T(1024)S(1)} %add_rsqrt_fusion.3, f32[4096]{0:T(1024)S(1)} %broadcast_multiply_fusion.3, bf16[2,1152,1152]{2,1,0:T(8,128)(2,1)} %param.31, ...), kind=kOutput, calls=%fused_computation.36.clone.clone.clone.2 | convolution fusion | flops 10966007808 | bytes 40449536 | tf_op jit(solution)/shard_map/rnd,df->rnf/dot_general | solution.py:38
  654.8 19.4 %fusion.41 = bf16[1,4096,1152]{2,1,0:T(8,128)(2,1)} fusion(bf16[2,1152,1152]{2,1,0:T(8,128)(2,1)} %param.32, bf16[4096,1152]{1,0:T(8,128)(2,1)} %fusion.31.clone.5), kind=kOutput, calls=%fused_computation.65 | convolution fusion | flops 10876354560 | bytes 21528576 | tf_op jit(solution)/shard_map/rnf,fd->rnd/dot_general | solution.py:39
  674.3 164.3 %all-reduce.11.cloned.1.call-done = bf16[1,4096,1152]{2,1,0:T(8,128)(2,1)} async-done(((bf16[1,4096,1152]{2,1,0:T(8,128)(2,1)}), bf16[1,4096,1152]{2,1,0:T(8,128)(2,1)}) %all-reduce.11.cloned.1.call-update) | async-done | bytes 9437200 | tf_op jit(solution)/shard_map/psum | solution.py:40
  838.6 20.6 %fusion.209 = (f32[4096]{0:T(1024)S(1)}, f32[1,4096,1152]{2,1,0:T(8,128)}) fusion(bf16[1,4096,1152]{2,1,0:T(8,128)(2,1)} %all-reduce.11.cloned.1.call-done, f32[1152]{0:T(1024)S(1)} %copy-done.14, bf16[1,4096,1152]{2,1,0:T(8,128)(2,1)} %all-reduce.9.cloned.1.call-done, bf16[1,4096,1152]{2,1,0:T(8,128)(2,1)} %all-reduce.7.cloned.1.call-done, ...), kind=kLoop, calls=%fused_computation.240 | loop fusion | flops 47181824 | bytes 56648704 | tf_op jit(solution)/shard_map/reduce_sum | solution.py:11
  867.8 16.5 fusion.62
  893.3 106.9 %fusion.219 = (f32[4,4096]{1,0:T(4,128)S(1)}, f32[4,4096,4096]{1,2,0:T(8,128)}) fusion(bf16[1,4096,3,4,72]{1,4,3,2,0:T(8,128)(2,1)} %convert_bitcast_fusion), kind=kOutput, calls=%fused_computation.248 | convolution fusion | flops 9865007104 | bytes 273219584 | tf_op jit(solution)/shard_map/sub | solution.py:22
  1000.3 83.3 %fusion.258 = bf16[4096,4,72]{0,2,1:T(8,128)(2,1)} fusion(f32[4,4096,4096]{1,2,0:T(8,128)} %get-tuple-element.38, f32[4,4096]{1,0:T(4,128)S(1)} %get-tuple-element.37, bf16[1,4096,3,4,72]{1,4,3,2,0:T(8,128)(2,1)} %convert_bitcast_fusion), kind=kOutput, calls=%bitcast_fusion.1.clone.2 | convolution fusion | flops 9799073792 | bytes 273219584 | tf_op jit(solution)/shard_map/rhqk,rkhd->rqhd/dot_general | solution.py:23
  1095.3 162.6 %all-reduce.13.cloned.1.call-done = bf16[1,4096,1152]{2,1,0:T(8,128)(2,1)} async-done(((bf16[1,4096,1152]{2,1,0:T(8,128)(2,1)}), bf16[1,4096,1152]{2,1,0:T(8,128)(2,1)}) %all-reduce.13.cloned.1.call-update) | async-done | bytes 9437200 | tf_op jit(solution)/shard_map/psum | solution.py:31
  1257.9 14.5 fusion.49
  1284.4 12.9 fusion.46
  1297.7 163.9 %all-reduce.15.cloned.1.call-done = bf16[1,4096,1152]{2,1,0:T(8,128)(2,1)} async-done(((bf16[1,4096,1152]{2,1,0:T(8,128)(2,1)}), bf16[1,4096,1152]{2,1,0:T(8,128)(2,1)}) %all-reduce.15.cloned.1.call-update) | async-done | bytes 9437200 | tf_op jit(solution)/shard_map/psum | solution.py:36
  1461.6 19.8 %fusion.208 = (f32[4096]{0:T(1024)S(1)}, f32[1,4096,1152]{2,1,0:T(8,128)}) fusion(bf16[1,4096,1152]{2,1,0:T(8,128)(2,1)} %all-reduce.15.cloned.1.call-done, f32[1,4096,1152]{2,1,0:T(8,128)} %get-tuple-element.22, bf16[1,4096,1152]{2,1,0:T(8,128)(2,1)} %all-reduce.13.cloned.1.call-done, f32[1152]{0:T(1024)S(1)} %copy-done.11), kind=kLoop, calls=%fused_computation.239 | loop fusion | flops 28307456 | bytes 56644096 | tf_op jit(solution)/shard_map/reduce_sum | solution.py:11
  1489.9 38.9 %fusion.42 = bf16[1,4096,1152]{2,1,0:T(8,128)(2,1)} fusion(f32[1,4096,1152]{2,1,0:T(8,128)} %get-tuple-element.20, f32[1152]{0:T(1024)S(1)} %copy-done.16, f32[1152]{0:T(1024)S(1)} %copy-done.17, f32[4096]{0:T(1024)S(1)} %add_rsqrt_fusion.1, f32[4096]{0:T(1024)S(1)} %broadcast_multiply_fusion.1, bf16[2,1152,1152]{2,1,0:T(8,128)(2,1)} %param.32, ...), kind=kOutput, calls=%fused_computation.66 | convolution fusion | flops 21814050816 | bytes 33661952 | tf_op jit(solution)/shard_map/rnf,fd->rnd/dot_general | solution.py:39
  1532.7 160.5 %all-reduce.17.cloned.1.call-done = bf16[1,4096,1152]{2,1,0:T(8,128)(2,1)} async-done(((bf16[1,4096,1152]{2,1,0:T(8,128)(2,1)}), bf16[1,4096,1152]{2,1,0:T(8,128)(2,1)}) %all-reduce.17.cloned.1.call-update) | async-done | bytes 9437200 | tf_op jit(solution)/shard_map/psum | solution.py:40
  1693.2 12.1 fusion.119
  1705.4 10.2 multiply_reduce_fusion.2
  (145 shorter events, 141.6 us)
Async XLA Ops:
  6.5 241.7 %copy-start = (bf16[1,120,1152]{2,1,0:T(8,128)(2,1)S(1)}, bf16[1,120,1152]{2,1,0:T(8,128)(2,1)}, u32[]{:S(2)}) copy-start(bf16[1,120,1152]{2,1,0:T(8,128)(2,1)} %param.19) | copy-start | bytes 829444
  6.5 405.7 %all-reduce.7.cloned.1.call-start = ((), (), s32[]{:S(2)}) async-start(), calls=%async_computation | async-start | bytes 18874368 | tf_op jit(solution)/shard_map/psum | solution.py:31
  151.8 83.4 %copy-start.25 = (bf16[2,4,72,1152]{3,2,1,0:T(8,128)(2,1)S(1)}, bf16[2,4,72,1152]{3,2,1,0:T(8,128)(2,1)}, u32[]{:S(2)}) copy-start(bf16[2,4,72,1152]{3,2,1,0:T(8,128)(2,1)} %param.27) | copy-start | bytes 3981316
  245.1 167.1 %copy-start.10 = (f32[1152]{0:T(1024)S(1)}, f32[1152]{0:T(1024)}, u32[]{:S(2)}) copy-start(f32[1152]{0:T(1024)} %get-tuple-element.39) | copy-start | bytes 13828
  245.2 364.5 %all-reduce.9.cloned.1.call-start = ((), (), s32[]{:S(2)}) async-start(), calls=%async_computation.1 | async-start | bytes 18874368 | tf_op jit(solution)/shard_map/psum | solution.py:36
  246.9 185.4 %copy-start.31 = (pred[120]{0:T(512)(128)(4,1)}, pred[120]{0:T(512)(128)(4,1)S(1)}, u32[]{:S(2)}) copy-start(pred[120]{0:T(512)(128)(4,1)S(1)} %iota_compare_fusion) | copy-start | bytes 364
  445.3 393.3 %all-reduce.11.cloned.1.call-start = ((), (), s32[]{:S(2)}) async-start(), calls=%async_computation.2 | async-start | bytes 18874368 | tf_op jit(solution)/shard_map/psum | solution.py:40
  609.7 11.9 copy-start.2
  609.7 22.2 %slice-start.5 = ((s8[9437184]{0:T(1024)(128)(4,1)}), s8[4194304]{0:T(1024)(128)(4,1)S(1)}, s32[]{:S(2)}) async-start(s8[9437184]{0:T(1024)(128)(4,1)} %bitcast.316), calls=%async_computation.11 | async-start | bytes 8388608
  609.7 22.2 %slice-start.6 = ((s8[9437184]{0:T(1024)(128)(4,1)}), s8[4194304]{0:T(1024)(128)(4,1)S(1)}, s32[]{:S(2)}) async-start(s8[9437184]{0:T(1024)(128)(4,1)} %bitcast.316), calls=%async_computation.12 | async-start | bytes 8388608
  674.2 164.4 %copy-start.14 = (f32[1152]{0:T(1024)S(1)}, f32[1152]{0:T(1024)}, u32[]{:S(2)}) copy-start(f32[1152]{0:T(1024)} %get-tuple-element.44) | copy-start | bytes 13828
  674.2 583.6 %all-reduce.13.cloned.1.call-start = ((), (), s32[]{:S(2)}) async-start(), calls=%async_computation.3 | async-start | bytes 18874368 | tf_op jit(solution)/shard_map/psum | solution.py:31
  1000.3 83.3 %copy-start.26 = (bf16[2,4,72,1152]{3,2,1,0:T(8,128)(2,1)S(1)}, bf16[2,4,72,1152]{3,2,1,0:T(8,128)(2,1)}, u32[]{:S(2)}) copy-start(bf16[2,4,72,1152]{3,2,1,0:T(8,128)(2,1)} %param.27) | copy-start | bytes 3981316
  1093.4 164.4 %copy-start.7 = (bf16[1,1152,4,72]{1,3,2,0:T(8,128)(2,1)S(1)}, bf16[1,1152,4,72]{1,3,2,0:T(8,128)(2,1)}, u32[]{:S(2)}) copy-start(bf16[1,1152,4,72]{1,3,2,0:T(8,128)(2,1)} %get-tuple-element.28) | copy-start | bytes 1990660
  1093.4 164.4 %copy-start.11 = (f32[1152]{0:T(1024)S(1)}, f32[1152]{0:T(1024)}, u32[]{:S(2)}) copy-start(f32[1152]{0:T(1024)} %get-tuple-element.10) | copy-start | bytes 13828
  1093.4 368.2 %all-reduce.15.cloned.1.call-start = ((), (), s32[]{:S(2)}) async-start(), calls=%async_computation.4 | async-start | bytes 18874368 | tf_op jit(solution)/shard_map/psum | solution.py:36
  1257.9 14.5 copy-start.32
  1297.2 396.0 %all-reduce.17.cloned.1.call-start = ((), (), s32[]{:S(2)}) async-start(), calls=%async_computation.5 | async-start | bytes 18874368 | tf_op jit(solution)/shard_map/psum | solution.py:40
  1528.8 164.4 %copy-start.13 = (f32[1152]{0:T(1024)S(1)}, f32[1152]{0:T(1024)}, u32[]{:S(2)}) copy-start(f32[1152]{0:T(1024)} %get-tuple-element.5) | copy-start | bytes 13828
  1693.2 12.1 copy-start.3
  1693.2 22.4 %slice-start = ((s8[18874368]{0:T(1024)(128)(4,1)}), s8[4194304]{0:T(1024)(128)(4,1)S(1)}, s32[]{:S(2)}) async-start(s8[18874368]{0:T(1024)(128)(4,1)} %bitcast.314), calls=%async_computation.6 | async-start | bytes 8388608
  1693.2 22.4 %slice-start.1 = ((s8[18874368]{0:T(1024)(128)(4,1)}), s8[4194304]{0:T(1024)(128)(4,1)S(1)}, s32[]{:S(2)}) async-start(s8[18874368]{0:T(1024)(128)(4,1)} %bitcast.314), calls=%async_computation.7 | async-start | bytes 8388608
  1693.2 22.4 %slice-start.2 = ((s8[18874368]{0:T(1024)(128)(4,1)}), s8[4194304]{0:T(1024)(128)(4,1)S(1)}, s32[]{:S(2)}) async-start(s8[18874368]{0:T(1024)(128)(4,1)} %bitcast.314), calls=%async_computation.8 | async-start | bytes 8388608
  1724.7 22.3 %copy-start.9 = (f32[1,128,128,4]{2,3,1,0:T(4,128)S(1)}, f32[1,128,128,4]{2,3,1,0:T(4,128)}, u32[]{:S(2)}) copy-start(f32[1,128,128,4]{2,3,1,0:T(4,128)} %param.23) | copy-start | bytes 786436
  (23 other events, 159.4 us)
Sparse Core Ops, SparseCore 0:
  245.3 166.8 all-reduce.6
  445.4 164.2 all-reduce.8
  674.3 164.2 all-reduce.10
  1093.6 164.2 all-reduce.12
  1297.4 164.2 all-reduce.14
  1528.9 164.2 all-reduce.16
where the time goes:
time: 1760 us; the launch traced here: 1750 us
  waiting for transfers between devices  977 us (56%)
  matrix products  593 us (34%)
  other arithmetic  129 us (7%)
  local copies, waits for them, and re-layouts  29.9 us (2%)
  between operations  17.6 us (1%)
    psum x2, waiting for transfers between devices, tp_block(): residual = residual + lax.psum(cross_part, 'tp').astype(jnp.float32)  328 us
    psum x2, waiting for transfers between devices, tp_block(): lax.psum(mlp_part, 'tp').astype(jnp.float32)  325 us
    psum x2, waiting for transfers between devices, tp_block(): lax.psum(self_part, 'tp').astype(jnp.float32)  324 us
    sub x4, matrix products, attention(): attn_prob = jax.nn.softmax(scores, axis=-1).astype(jnp.bfloat16)  224 us
    dot_general x2, matrix products, attention(): jnp.einsum('rhqk,rkhd->rqhd', attn_prob, values, preferred_element_type=j...  167 us
    reduce_sum x5, other arithmetic, layer_norm(): mean_val = jnp.mean(values, axis=-1, keepdims=True)  69.5 us
    dot_general x2, matrix products, tp_block(): jnp.einsum('rnf,fd->rnd', mlp_hidden, w_fc2, preferred_element_type=jnp.f...  58.2 us
    unnamed x6, matrix products  56 us
  transfers between devices with their start and end apart: 6, of which 6 were waited for; matrix products, arithmetic and copies ran while one was open for 0% of the time, Pallas kernels for 0%

commit v1 on v0

v1 whole, which is shorter than its diff:
```python
import functools
import math

import jax
import jax.numpy as jnp
from jax import lax
from jax.experimental import pallas as pl
from jax.experimental.pallas import tpu as pltpu
from jax.sharding import PartitionSpec as P

GUIDANCE = 4.5
LN_EPS = 1e-6
HD = 72
NH = 4
TP = 4
F32 = jnp.float32
BF16 = jnp.bfloat16
QK_SCALE = HD ** -0.5
QK_EXP2 = QK_SCALE * math.log2(math.e)
SAFE_EXP2 = 48.0
SAFE_V = 2.0 ** 40
VMEM = 60 * 2 ** 20
HBM = pl.BlockSpec(memory_space=pltpu.HBM)
MESH = pl.DeviceIdType.MESH
DOWN, ALONG = [dict(axis=axis, keepdims=True) for axis in range(2)]
PROJ, CQ, CPROJ, FC1, FC2A, FC2B = WEIGHTS = range(6)
SMALL = (PROJ, CQ, CPROJ)
PLACES = ('own', 'near', 'far_a', 'far_b', 'rest_a', 'rest_b')


def dot(a, b, dims='nn'):
    dims = {'nn': ((1,), (0,)), 'nt': ((1,), (1,)), 'tn': ((0,), (0,))}[dims]
    return lax.dot_general(a, b, (dims, ((), ())), preferred_element_type=F32)


def row(ref, i):
    return ref[pl.ds(i, 1)]


def layer_norm(values):
    mean_val = jnp.mean(values, **ALONG)
    centered = values - mean_val
    variance = jnp.mean(centered * centered, **ALONG)
    return centered * lax.rsqrt(variance + LN_EPS)


def where_am_i():
    t, y = lax.axis_index('tp'), lax.axis_index('cfg')
    return t, y, lax.rem(t, 2)


def target(kind):
    t, y, c = where_am_i()
    return {
        'core': {'tp': t + 1 - 2 * c, 'cfg': y},
        'x': {'tp': lax.rem(t + 2, 4), 'cfg': y},
        'diag': {'tp': 3 - t, 'cfg': y},
        'y': {'tp': t, 'cfg': 1 - y},
    }[kind]


def guarded(cond, fn):
    if cond == 'all':
        fn()
        return
    _, y, c = where_am_i()
    pl.when(c == y if cond == 'same' else c != y)(fn)


def receiver(kind, cond):
    if cond == 'all' or kind in ('x', 'diag'):
        return cond
    return 'diff' if cond == 'same' else 'same'


def greet():
    barrier = pltpu.get_barrier_semaphore()
    for kind in ('core', 'x', 'diag', 'y'):
        pl.semaphore_signal(barrier, inc=1, device_id=target(kind), device_id_type=MESH)
    pl.semaphore_wait(barrier, 4)


class Comm:
    def __init__(self, ops, refs, sems):
        self.ops, self.refs, self.sems = ops, refs, sems
        self.left = {op[1] for op in ops}

    def descriptor(self, i):
        src, dst, kind, cond = self.ops[i]
        return pltpu.make_async_remote_copy(
            src_ref=self.refs[src], dst_ref=self.refs[dst], send_sem=self.sems.at[0, i], recv_sem=self.sems.at[1, i],
            device_id=target(kind), device_id_type=MESH)

    def start(self, ops):
        for i, op in enumerate(self.ops):
            if op in ops:
                guarded(op[3], lambda: self.descriptor(i).start())

    def arrive(self, name):
        if name in self.left:
            self.left.remove(name)
            i = [op[1] for op in self.ops].index(name)
            guarded(receiver(*self.ops[i][2:]), lambda: self.descriptor(i).wait_recv())

    def finish(self):
        for i, op in enumerate(self.ops):
            guarded(op[3], lambda: self.descriptor(i).wait_send())
            self.arrive(op[1])


class Buffers:
    def __init__(self):
        self.arrays = {}

    def put(self, name, array, shape=(), index=()):
        self.arrays[name] = array, shape or array.shape, index

    def take(self, made, outs):
        for name, array in zip(made, outs):
            self.put(name, array)

    def plan(self, ops):
        made = [op[1] for op in ops]
        read = []
        for op in ops:
            if op[0] not in made and op[0] not in read:
                read.append(op[0])
        return read, made

    def shape(self, name, ops):
        for src, dst, _, _ in ops:
            if dst == name:
                return self.shape(src, ops)
        return self.arrays[name][1]

    def operands(self, names):
        return [self.arrays[n][0] for n in names]

    def bind(self, read, made, in_refs, out_refs):
        refs = {}
        for n, ref in zip(read, in_refs):
            index = self.arrays[n][2]
            refs[n] = ref.at[index] if index else ref
        refs.update(zip(made, out_refs))
        return refs


def comm_params(cid, n_ops):
    return dict(
        sems=pltpu.SemaphoreType.DMA((2, n_ops)),
        params=pltpu.CompilerParams(vmem_limit_bytes=VMEM, collective_id=cid, has_side_effects=True),
    )


def qkv(bufs, x, mods, w_rows, w_heads, layer, gather, ops, cid):
    d = x.shape[1]
    n = x.shape[0] * (TP if gather else 1)
    blk = n // TP
    piece = NH * HD
    moves = [('a', 'a1', 'core', 'all'), ('a', 'a2', 'x', 'all'), ('a2', 'a3', 'core', 'all')] if gather else []
    bufs.put('a', x)
    all_ops = moves + ops
    read, made = bufs.plan(all_ops)
    if 'a' not in read:
        read = ['a'] + read
    n_in = 4 + len(read)

    def body(*refs):
        mod_ref, wq_ref, wk_ref, wv_ref = refs[:4]
        q_ref, k_ref, v_ref, n_ref = refs[n_in:n_in + 4]
        named = bufs.bind(read, made, refs[4:n_in], refs[n_in + 4:n_in + 4 + len(made)])
        xbuf, wqv, wk, lsem, sems = refs[n_in + 4 + len(made):]
        comm = Comm(all_ops, named, sems)
        step = pl.program_id(0)
        t, y, c = where_am_i()
        owners = [t, t + 1 - 2 * c, lax.rem(t + 2, 4), 3 - t]

        def load(s):
            src = named[['a', 'a1', 'a2', 'a3'][s]] if gather else named['a'].at[pl.ds(owners[s] * blk, blk)]
            return pltpu.make_async_copy(src, xbuf.at[s % 2], lsem.at[s % 2])

        for s in range(TP):
            @pl.when(step == s)
            def _():
                if s == 0:
                    load(0).start()
                    greet()
                    wqv[0:piece] = wq_ref[...]
                    wqv[piece:2 * piece] = wv_ref[...]
                    for h in range(NH):
                        head = jnp.concatenate([wk_ref[h].astype(F32), jnp.zeros((128 - HD, d), F32)], axis=0)
                        wk[h * 128:(h + 1) * 128] = head.astype(BF16)
                    comm.start([op for op in all_ops if op not in moves[2:]])
                if gather:
                    if s:
                        comm.arrive('a%d' % s)
                    if s == 2:
                        comm.start(moves[2:])
                    if s:
                        load(s).start()
                elif s + 1 < TP:
                    load(s + 1).start()
                load(s).wait()

        x = xbuf[lax.rem(step, 2)]
        a = x
        if not gather:
            shift, scale = row(mod_ref, 6 * layer), row(mod_ref, 6 * layer + 1)
            a = (layer_norm(x.astype(F32)) * (1.0 + scale) + shift).astype(BF16)
        qv = dot(wqv[...], a, 'nt')
        q, v = qv[:piece], qv[piece:]
        norms = []
        for h in range(NH):
            qh = q[h * HD:(h + 1) * HD].astype(BF16).astype(F32)
            q_ref[h] = jnp.concatenate([qh, jnp.zeros((128 - HD, blk), F32)], axis=0).astype(BF16)
            norms.append(jnp.max(jnp.sum(qh * qh, **DOWN), **ALONG))
        kb = dot(a, wk[...], 'nt').astype(BF16)
        k_ref[...] = kb
        for h in range(NH):
            kh = kb[:, h * 128:(h + 1) * 128].astype(F32)
            norms.append(jnp.max(jnp.sum(kh * kh, **ALONG), **DOWN))
        for h in range(NH):
            v_ref[h] = v[h * HD:(h + 1) * HD].astype(BF16)
        norms.append(jnp.max(jnp.max(jnp.abs(v), **DOWN), **ALONG))
        n_ref[0] = jnp.concatenate([jnp.broadcast_to(m, (1, 128)) for m in norms] + [jnp.zeros((7, 128), F32)], axis=0)

        @pl.when(step == TP - 1)
        def _():
            comm.finish()

    extra = comm_params(cid, len(all_ops))
    out = pl.pallas_call(
        body,
        grid=(TP,),
        in_specs=[
            pl.BlockSpec(mods.shape, lambda i: (0, 0)),
            pl.BlockSpec((None, None, piece, d), lambda i: (layer, 0, 0, 0)),
            pl.BlockSpec((None, None, NH, HD, d), lambda i: (layer, 1, 0, 0, 0)),
            pl.BlockSpec((None, None, piece, d), lambda i: (layer, 2, 0, 0)),
        ] + [HBM] * len(read),
        out_specs=[
            pl.BlockSpec((NH, 128, blk), lambda i: (0, 0, i)),
            pl.BlockSpec((blk, NH * 128), lambda i: (i, 0)),
            pl.BlockSpec((NH, HD, blk), lambda i: (0, 0, i)),
            pl.BlockSpec((1, 16, 128), lambda i: (i, 0, 0)),
        ] + [HBM] * len(made),
        out_shape=[
            jax.ShapeDtypeStruct((NH, 128, n), BF16),
            jax.ShapeDtypeStruct((n, NH * 128), BF16),
            jax.ShapeDtypeStruct((NH, HD, n), BF16),
            jax.ShapeDtypeStruct((TP, 16, 128), F32),
        ] + [jax.ShapeDtypeStruct(bufs.shape(m, all_ops), BF16) for m in made],
        scratch_shapes=[
            pltpu.VMEM((2, blk, d), BF16), pltpu.VMEM((2 * piece, d), BF16), pltpu.VMEM((NH * 128, d), BF16),
            pltpu.SemaphoreType.DMA((2,)), extra['sems'],
        ],
        compiler_params=extra['params'],
        name='qkv_%d' % cid,
    )(mods, w_rows, w_heads, w_rows, *bufs.operands(read))
    bufs.take(made, out[4:])
    return out[:4]


def attention(bufs, q, k, v, first, ops, cid, bq=1024, bk=512):
    n = k.shape[0]
    own = n // TP
    per = own // bq
    read, made = bufs.plan(ops)
    steps = (NH, 2 * per)

    def body(*refs):
        q_ref, k_ref, v_ref = refs[:3]
        o_ref = refs[3 + len(read)]
        named = bufs.bind(read, made, refs[3:3 + len(read)], refs[4 + len(read):4 + len(read) + len(made)])
        comm = Comm(ops, named, refs[-1])
        head, block = pl.program_id(0), pl.program_id(1)

        @pl.when((head == 0) & (block == 0))
        def _():
            greet()
            comm.start(ops)

        def score(j):
            return dot(k_ref[j * bk:(j + 1) * bk], q_ref[0])

        s = score(0)
        total = jnp.zeros((8, bq), F32)
        acc = jnp.zeros((HD, bq), F32)
        for j in range(n // bk):
            if j + 1 < n // bk:
                ahead = score(j + 1)
            p = jnp.exp2(s * QK_EXP2)
            part = jnp.sum(p.reshape(bk // 8, 8, bq), axis=0)
            mix = dot(v_ref[0, :, j * bk:(j + 1) * bk], p.astype(BF16))
            total, acc = total + part, acc + mix
            s = ahead
        o_ref[0, 0] = (acc / jnp.sum(total, **DOWN)).astype(BF16)

        @pl.when((head == steps[0] - 1) & (block == steps[1] - 1))
        def _():
            comm.finish()

    extra = comm_params(cid, len(ops))
    out = pl.pallas_call(
        body,
        grid=steps,
        in_specs=[
            pl.BlockSpec((1, 128, bq), lambda h, i: (h, 0, first * per + i)),
            pl.BlockSpec((n, 128), lambda h, i: (0, h)),
            pl.BlockSpec((1, HD, n), lambda h, i: (h, 0, 0)),
        ] + [HBM] * len(read),
        out_specs=[pl.BlockSpec((1, 1, HD, bq), lambda h, i: (i // per, h, 0, i % per))] + [HBM] * len(made),
        out_shape=[jax.ShapeDtypeStruct((2, NH, HD, own), BF16)]
        + [jax.ShapeDtypeStruct(bufs.shape(m, ops), BF16) for m in made],
        scratch_shapes=[extra['sems']],
        compiler_params=extra['params'],
        name='attn_%d' % cid,
    )(q, k, v, *bufs.operands(read))
    bufs.take(made, out[1:])
    return out[0]


def repair_body(n_ref, q_hbm, k_hbm, v_hbm, o_hbm, out_hbm, q_ref, k_ref, v_ref, o_ref, sems, *, first):
    big = jnp.max(n_ref[...], axis=0)
    bound = jnp.max(jnp.sqrt(big[0:4]) * jnp.sqrt(big[4:8])) * QK_EXP2
    own = o_hbm.shape[3]
    bq = q_ref.shape[1]
    n = k_ref.shape[0]

    @pl.when(jnp.logical_not((bound < SAFE_EXP2) & (jnp.max(big[8:9]) < SAFE_V)))
    def _():
        @pl.loop(0, NH)
        def _(h):
            col = pl.multiple_of(h * 128, 128)
            ins = [pltpu.make_async_copy(k_hbm.at[:, pl.ds(col, 128)], k_ref, sems.at[0]),
                   pltpu.make_async_copy(v_hbm.at[h], v_ref, sems.at[1])]
            for cp in ins:
                cp.start()
            for cp in ins:
                cp.wait()

            @pl.loop(0, 2 * own // bq)
            def _(i):
                cp = pltpu.make_async_copy(q_hbm.at[h, :, pl.ds(pl.multiple_of(first * own + i * bq, bq), bq)], q_ref, sems.at[2])
                cp.start()
                cp.wait()

                def step(j, carry):
                    top, total, acc = carry
                    row = pl.multiple_of(j * bq, bq)
                    s = dot(k_ref[pl.ds(row, bq)], q_ref[...])
                    high = jnp.maximum(top, jnp.max(s, **DOWN))
                    p = jnp.exp2((s - high) * QK_EXP2)
                    shrink = jnp.exp2((top - high) * QK_EXP2)
                    mix = dot(v_ref[:, pl.ds(row, bq)], p.astype(BF16))
                    return high, total * shrink + jnp.sum(p, **DOWN), acc * shrink + mix

                start = (jnp.full((1, bq), -3e38, F32), jnp.zeros((1, bq), F32), jnp.zeros((HD, bq), F32))
                _, total, acc = lax.fori_loop(0, n // bq, step, start)
                o_ref[...] = (acc / total).astype(BF16)
                dst = out_hbm.at[i // (own // bq), h, :, pl.ds(pl.multiple_of((i % (own // bq)) * bq, bq), bq)]
                cp = pltpu.make_async_copy(o_ref, dst, sems.at[3])
                cp.start()
                cp.wait()


def repair(norms, q, k, v, o, first, bq=512):
    n = k.shape[0]
    return pl.pallas_call(
        functools.partial(repair_body, first=first),
        in_specs=[pl.BlockSpec(memory_space=pltpu.VMEM)] + [HBM] * 4,
        out_specs=HBM,
        out_shape=jax.ShapeDtypeStruct(o.shape, o.dtype),
        scratch_shapes=[
            pltpu.VMEM((128, bq), BF16), pltpu.VMEM((n, 128), BF16), pltpu.VMEM((HD, n), BF16), pltpu.VMEM((HD, bq), BF16),
            pltpu.SemaphoreType.DMA((4,)),
        ],
        input_output_aliases={4: 0},
        compiler_params=pltpu.CompilerParams(vmem_limit_bytes=VMEM),
        name='repair',
    )(norms, q, k, v, o)


def tail(bufs, cap_len, x, o_own, o_far, o_rest, mods, cross, w_out, b_out, layer, last, plan, cid, bt=512):
    d = x.shape[1]
    n = o_own.shape[2]
    piece = NH * HD
    ops = [('o1', 'o1_in', 'core', 'all')] + plan[0] + plan[1] + plan[2]
    made = [op[1] for op in ops[1:]]
    read = [m for m in [(p, layer, w) for p in PLACES for w in WEIGHTS] if m not in made]
    read += [op[0] for op in ops[1:] if op[0] not in read + made]
    n_vmem = 8
    n_in = n_vmem + 4 + len(read)
    n_out = 1 if last else 2

    def body(*refs):
        s_ref, mod_ref, c0, c1, c2, c3, wout_ref, bout_ref, x_hbm, oo, of, orr = refs[:n_vmem + 4]
        outs = refs[n_in:n_in + n_out]
        named = bufs.bind(read, made, refs[n_vmem + 4:n_in], refs[n_in + n_out:n_in + n_out + len(made)])
        scratch = refs[n_in + n_out + len(made):]
        if last:
            xs, ms, scratch = scratch[0], scratch[1], scratch[2:]
            x_in = xs
        else:
            xs, ms = outs
            x_in, scratch = scratch[0], scratch[1:]
        os, wp, wcq, wcp, w1, w2, part, heads, lsem, osem, sems = scratch
        named['o1'] = oo.at[1]
        named['o1_in'] = os.at[piece:2 * piece]
        comm = Comm(ops, named, sems)
        c_refs = (c0, c1, c2, c3)

        def place(w, r):
            if w in SMALL:
                return (wp, wcq, wcp)[w].at[r * piece:(r + 1) * piece]
            if w == FC1:
                return w1.at[r % 2]
            return w2.at[r % 2, 0:d // 2] if w == FC2A else w2.at[r % 2, d // 2:d]

        def copy(name, w, r):
            return pltpu.make_async_copy(named[(name, layer, w)], place(w, r), lsem.at[w, r])

        def fetch(w, r):
            if r < 2:
                copy(PLACES[r], w, r).start()
                return
            for cond, name in zip(('same', 'diff'), PLACES[2 * r - 2:2 * r]):
                comm.arrive((name, layer, w))
                guarded(cond, copy(name, w, r).start)

        def ready(w, r):
            copy(PLACES[0], w, r).wait()

        t, _, _ = where_am_i()
        x_from = x_hbm if last else x_hbm.at[pl.ds(t * n, n)]
        pieces = [(oo.at[0], os.at[0:piece]), (of, os.at[2 * piece:3 * piece]), (orr, os.at[3 * piece:4 * piece]), (x_from, x_in)]
        loads = [pltpu.make_async_copy(src, dst, osem.at[i]) for i, (src, dst) in enumerate(pieces)]
        for cp in loads:
            cp.start()
        greet()
        comm.start(ops[:1] + plan[0])
        for w in SMALL:
            for r in range(TP):
                fetch(w, r)
        for cp in loads:
            cp.wait()
        comm.arrive('o1_in')
        for w in SMALL:
            for r in range(TP):
                ready(w, r)
        for r in range(2):
            for w in (FC1, FC2A, FC2B):
                fetch(w, r)

        gate1, shift2, scale2, gate2, shift3, scale3 = [row(mod_ref, 6 * layer + i) for i in range(2, 8)]
        keys = lax.broadcasted_iota(jnp.int32, (128, bt), 0) < s_ref[0]

        @pl.loop(0, n // bt)
        def _(b):
            rows = pl.ds(pl.multiple_of(b * bt, bt), bt)
            y = dot(os[:, rows], wp[...], 'tn')
            x = x_in[rows, :].astype(F32) + gate1 * y.astype(BF16).astype(F32)
            q = dot(wcq[...], x.astype(BF16), 'nt')
            for r in range(TP):
                scores = []
                for h in range(NH):
                    row = (r * NH + h) * HD
                    s = dot(c_refs[r][h], q[row:row + HD].astype(BF16), 'tn') * QK_SCALE
                    scores.append(jnp.where(keys, s, -1e30))
                probs = [jnp.exp(s - jnp.max(s, **DOWN)) for s in scores]
                totals = [jnp.sum(p, **DOWN) for p in probs]
                mixes = [dot(c_refs[r][NH + h], probs[h].astype(BF16)) for h in range(NH)]
                mixes = [m / total for m, total in zip(mixes, totals)]
                heads[r * piece:(r + 1) * piece] = jnp.concatenate(mixes, axis=0).astype(BF16)
            z = dot(heads[...], wcp[...], 'tn')
            x = x + z.astype(BF16).astype(F32)
            xs[rows, :] = x
            ms[rows, :] = (layer_norm(x) * (1.0 + scale2) + shift2).astype(BF16)

        for op in plan[1]:
            comm.arrive(op[0])
        comm.start(plan[1])

        @pl.loop(0, TP)
        def _(r):
            slot = lax.rem(r, 2)
            for s in range(TP):
                @pl.when(r == s)
                def _():
                    for w in (FC1, FC2A, FC2B):
                        ready(w, s)

            @pl.loop(0, n // bt)
            def _(b):
                rows = pl.ds(pl.multiple_of(b * bt, bt), bt)
                m = ms[rows, :]
                cuts = ((0, 512), (512, d))
                us = [dot(m, w1[slot, :, lo:hi]) for lo, hi in cuts]
                sums = []
                for u, (lo, hi) in zip(us, cuts):
                    half = 0.5 * u
                    g = half + half * jnp.tanh(u * (GELU0 + GELU1 * (u * u)))
                    sums.append(dot(g.astype(BF16), w2[slot, lo:hi, :]))
                add = sums[0] + sums[1]

                @pl.when(r == 0)
                def _():
                    part[rows, :] = add

                @pl.when(r > 0)
                def _():
                    part[rows, :] += add

            @pl.when(r == 0)
            def _():
                fetch(FC1, 2)
                if last:
                    fetch(FC2A, 2)
                    fetch(FC2B, 2)

            @pl.when(r == 1)
            def _():
                for op in plan[2]:
                    comm.arrive(op[0])
                comm.start(plan[2])
                if not last:
                    fetch(FC2A, 2)
                    fetch(FC2B, 2)
                fetch(FC1, 3)
                fetch(FC2A, 3)
                if last:
                    fetch(FC2B, 3)

            if not last:
                @pl.when(r == 2)
                def _():
                    fetch(FC2B, 3)

        @pl.loop(0, n // bt)
        def _(b):
            rows = pl.ds(pl.multiple_of(b * bt, bt), bt)
            x = xs[rows, :] + gate2 * part[rows, :].astype(BF16).astype(F32)
            a = (layer_norm(x) * (1.0 + scale3) + shift3).astype(BF16)
            if last:
                outs[0][:, rows] = dot(wout_ref[...], a, 'nt') + bout_ref[:, 0:1]
            else:
                xs[rows, :] = x
                ms[rows, :] = a

        comm.finish()

    vm = pl.BlockSpec(memory_space=pltpu.VMEM)
    if last:
        out_shape = [jax.ShapeDtypeStruct((w_out.shape[0], n), F32)]
        scratch = [pltpu.VMEM((n, d), F32), pltpu.VMEM((n, d), BF16)]
    else:
        out_shape = [jax.ShapeDtypeStruct((n, d), F32), jax.ShapeDtypeStruct((n, d), BF16)]
        scratch = [pltpu.VMEM((n, d), BF16)]
    extra = comm_params(cid, len(ops))
    square = pltpu.VMEM((d, d), BF16)
    pair = pltpu.VMEM((2, d, d), BF16)
    of_layer = pl.BlockSpec((None, *cross[0].shape[1:]), lambda i: (layer, 0, 0, 0))
    out = pl.pallas_call(
        body,
        grid=(1,),
        in_specs=[pl.BlockSpec(memory_space=pltpu.SMEM), vm] + [of_layer] * TP + [vm, vm] + [HBM] * (4 + len(read)),
        out_specs=[vm] * n_out + [HBM] * len(made),
        out_shape=out_shape + [jax.ShapeDtypeStruct(bufs.shape(m, ops), BF16) for m in made],
        scratch_shapes=scratch + [
            pltpu.VMEM((d, n), BF16), square, square, square, pair, pair, pltpu.VMEM((n, d), F32), pltpu.VMEM((d, bt), BF16),
            pltpu.SemaphoreType.DMA((len(WEIGHTS), TP)), pltpu.SemaphoreType.DMA((TP,)), extra['sems'],
        ],
        compiler_params=extra['params'],
        name='tail_%d' % cid,
    )(cap_len, mods, *cross, w_out, b_out, x, o_own, o_far, o_rest, *bufs.operands(read))
    bufs.take(made, out[n_out:])
    return out[:n_out]


def split3(v):
    high = v.astype(BF16)
    rest = v - high.astype(F32)
    mid = rest.astype(BF16)
    return high, mid, (rest - mid.astype(F32)).astype(BF16)


def finish(tokens, x_t, alpha_bar, cid):
    total, lanes = x_t.shape
    own = total // TP
    peers = ('core', 'x', 'diag')

    def body(tok_ref, x_ref, ab_ref, out_ref, mine, other, sems):
        t, y, _ = where_am_i()
        greet()
        cols = lax.broadcasted_iota(jnp.int32, (lanes, 2 * lanes), 1)
        twice = 2 * lax.broadcasted_iota(jnp.int32, (lanes, 2 * lanes), 0)
        terms = []
        for q in range(2):
            rows = [tok_ref[16 * p + 8 * q:16 * p + 8 * q + 8, k * lanes:(k + 1) * lanes] for k in range(8) for p in range(2)]
            pick = (cols == twice + q).astype(F32).astype(BF16)
            for part in split3(jnp.concatenate(rows, axis=0)):
                terms.append(dot(part, pick))
        wide = sum(terms[1:], terms[0])
        for k in range(8):
            for odd in range(2):
                half = wide[16 * k:16 * k + 16, odd * lanes:(odd + 1) * lanes]
                mine[16 * k + 8 * odd:16 * k + 8 * odd + 8] = jnp.concatenate([half[0:4], half[8:12]], axis=0)
        swap = pltpu.make_async_remote_copy(
            src_ref=mine, dst_ref=other, send_sem=sems.at[0, 3], recv_sem=sems.at[1, 3],
            device_id=target('y'), device_id_type=MESH)
        swap.start()
        swap.wait()
        cond, uncond = jnp.where(y == 0, mine[...], other[...]), jnp.where(y == 0, other[...], mine[...])
        guided = uncond + GUIDANCE * (cond - uncond)
        abar_t, abar_prev = ab_ref[0:1, 0:1], ab_ref[0:1, 1:2]
        rows = pl.ds(pl.multiple_of(t * own, own), own)
        x_zero = (x_ref[rows] - jnp.sqrt(1.0 - abar_t) * guided) / jnp.sqrt(abar_t)
        out_ref[rows] = jnp.sqrt(abar_prev) * x_zero + jnp.sqrt(1.0 - abar_prev) * guided
        sends = [pltpu.make_async_remote_copy(
            src_ref=out_ref.at[rows], dst_ref=out_ref.at[rows], send_sem=sems.at[0, i], recv_sem=sems.at[1, i],
            device_id=target(kind), device_id_type=MESH) for i, kind in enumerate(peers)]
        for cp in sends:
            cp.start()
        for cp in sends:
            cp.wait()

    vm = pl.BlockSpec(memory_space=pltpu.VMEM)
    return pl.pallas_call(
        body,
        in_specs=[vm] * 3,
        out_specs=vm,
        out_shape=jax.ShapeDtypeStruct(x_t.shape, F32),
        scratch_shapes=[pltpu.VMEM((own, lanes), F32), pltpu.VMEM((own, lanes), F32), pltpu.SemaphoreType.DMA((2, 4))],
        compiler_params=pltpu.CompilerParams(collective_id=cid, has_side_effects=True),
        name='finish',
    )(tokens, x_t, alpha_bar)


GELU0 = math.sqrt(2.0 / math.pi)
GELU1 = GELU0 * 0.044715


def over_x(layer, ws):
    return [(('own', layer, w), ('far_a', layer, w), 'x', 'same') for w in ws]


def to_core(layer, ws):
    return [(('own', layer, w), ('near', layer, w), 'core', 'all') for w in ws]


def forward(layer, ws):
    return [op for w in ws for op in (
        (('far_a', layer, w), ('far_b', layer, w), 'y', 'same'), (('far_a', layer, w), ('rest_b', layer, w), 'core', 'same'))]


def hand_on(layer, ws):
    return [(('far_b', layer, w), ('rest_a', layer, w), 'core', 'diff') for w in ws]


def solution(mesh):
    row_spec = P(('dp', 'cfg'))
    part_spec = P('dp')
    tp1, tp2, tp3 = [P(*(None,) * i, 'tp') for i in range(1, 4)]
    in_specs = (row_spec, row_spec, row_spec, part_spec, part_spec, part_spec, part_spec, P(),
                tp3, tp1, tp2, tp3, tp1, tp2, tp1, P(), P(), P())

    def local_step(hidden, caption, cap_len, t_block, t_embed, x_t, alpha_bar, mod_table, w_qkv, w_proj, w_cq, w_ckv, w_cproj, w_fc1, w_fc2, final_table, w_out, b_out):
        n, d = hidden.shape[1:]
        own_n = n // TP
        layers = mod_table.shape[0]

        w_heads = w_qkv.transpose(0, 2, 3, 4, 1)
        w_rows = w_heads.reshape(layers, 3, NH * HD, d)
        by_rows = lambda w: w.reshape(layers, NH * HD, d)
        owned = (by_rows(w_proj), by_rows(w_cq.transpose(0, 2, 3, 1)), by_rows(w_cproj), w_fc1)
        bufs = Buffers()
        for layer in range(layers):
            for w, array in enumerate(owned):
                bufs.put(('own', layer, w), array, array.shape[1:], (layer,))
            for half in range(2):
                index = (layer, slice(half * d // 2, (half + 1) * d // 2))
                bufs.put(('own', layer, FC2A + half), w_fc2, (d // 2, d), index)

        base = jnp.concatenate([t_block.reshape(6, d), t_block.reshape(6, d), t_embed, t_embed])
        mods = jnp.concatenate([mod_table.reshape(6 * layers, d), final_table]).astype(F32) + base.astype(F32)
        bout = jnp.broadcast_to(b_out.astype(F32)[:, None], (b_out.shape[0], 128))

        cap = jnp.pad(caption[0], ((0, 128 - caption.shape[1]), (0, 0)))
        ckv_t = w_ckv.transpose(0, 2, 3, 4, 1).reshape(layers * 2 * NH * HD, d)
        ckv = dot(ckv_t, cap, 'nt').astype(BF16).reshape(layers, 2 * NH, HD, 128)
        bufs.put('c', ckv)

        plans = [
            (to_core(0, WEIGHTS) + over_x(0, SMALL) + [('c', 'c1', 'core', 'all')],
             over_x(0, [FC1]) + forward(0, SMALL) + [('c', 'c2', 'x', 'all')],
             over_x(0, [FC2A]) + forward(0, [FC1]) + hand_on(0, SMALL) + [('c2', 'c3', 'core', 'all')],
             (over_x(0, [FC2B]) + forward(0, [FC2A]) + hand_on(0, [FC1]) + over_x(1, [FC1, PROJ, CQ]) + to_core(1, WEIGHTS),
              forward(0, [FC2B]) + hand_on(0, [FC2A]), hand_on(0, [FC2B]))),
            (over_x(1, [CPROJ]) + forward(1, [PROJ, CQ, FC1]),
             over_x(1, [FC2A, FC2B]) + forward(1, [CPROJ]) + hand_on(1, [PROJ, CQ, FC1]),
             forward(1, [FC2A, FC2B]) + hand_on(1, [CPROJ]),
             (hand_on(1, [FC2A, FC2B]), [], [])),
        ]
        x = a = hidden[0]
        for layer in range(layers):
            p_qkv, p_other, p_own, p_tail = plans[layer]
            cid = 1 + 4 * layer
            q, k, v, norms = qkv(bufs, a, mods, w_rows, w_heads, layer, layer > 0, p_qkv, cid)
            o = attention(bufs, q, k, v, 2, p_other, cid + 1)
            o = repair(norms, q, k, v, o, 2).reshape(2, NH * HD, own_n)
            for i in range(2):
                bufs.put(('o', layer, i), o, o.shape[1:], (i,))
            send = [(('o', layer, i), ('o_in', layer, i), kind, 'all') for i, kind in enumerate(('x', 'diag'))]
            o = attention(bufs, q, k, v, 0, send + p_own, cid + 2)
            o = repair(norms, q, k, v, o, 0).reshape(2, NH * HD, own_n)
            o_far, o_rest = [bufs.arrays[('o_in', layer, i)][0] for i in range(2)]
            cross = [bufs.arrays[m][0] for m in ('c', 'c1', 'c2', 'c3')]
            out = tail(bufs, cap_len, x, o, o_far, o_rest, mods, cross, w_out.T, bout, layer, layer == layers - 1, p_tail, cid + 3)
            x, a = out[0], out[-1]
        pixels = x_t.transpose(0, 1, 3, 2).reshape(-1, x_t.shape[2])
        x_prev = finish(x, pixels, alpha_bar, cid + 4)
        return x_prev.reshape(1, x_t.shape[1], x_t.shape[3], x_t.shape[2]).transpose(0, 1, 3, 2)

    return jax.shard_map(local_step, mesh=mesh, in_specs=in_specs, out_specs=part_spec, check_vma=False)
```

time: 1760 us -> 411 us (0.23)
  waiting for transfers between devices: 977 us -> 0 us
  matrix products: 593 us -> 1.87 us
  Pallas kernels: 0 us -> 393 us
  other arithmetic: 129 us -> 2.26 us
  local copies, waits for them, and re-layouts: 29.9 us -> 5.66 us
    psum x6 -> x0, waiting for transfers between devices: 977 us -> none  [the longest x2 328 us: tp_block(): residual = residual + lax.psum(cross_part, 'tp').astype(jnp.float32)]
    pallas_call x0 -> x13, Pallas kernels: none -> 393 us  [the longest x4 154 us: attention(): pl.pallas_call(body, grid=steps, in_specs=[pl.BlockSpec((1, 128, bq), lam...]
    dot_general x12 -> x1, matrix products: 312 us -> 1.87 us  [dot(): return lax.dot_general(a, b, (dims, ((), ())), preferred_element_type=F32)]
    sub x4 -> x0, matrix products: 224 us -> none  [attention(): attn_prob = jax.nn.softmax(scores, axis=-1).astype(jnp.bfloat16)]
    reduce_sum x10 -> x0, other arithmetic: 109 us -> none  [the longest x5 69.5 us: layer_norm(): mean_val = jnp.mean(values, axis=-1, keepdims=True)]
    unnamed x6 -> x0, matrix products: 56 us -> none
    convert_element_type x5 -> x0, other arithmetic: 18.1 us -> none  [the longest x2 18 us: tp_block(): jnp.einsum('rnd,dshe->rnshe', attn_in, w_qkv, preferred_element_type=jnp....]
  transfers between devices with their start and end apart: 6 -> 0, of which waited for: 6 -> 0; matrix products, arithmetic and copies ran while one was open for 0% -> 0% of each run, Pallas kernels for 0% -> 0%
where the time goes in v1:
time: 411 us; the launch traced here: 404 us
  Pallas kernels  393 us (96%)
  local copies, waits for them, and re-layouts  5.66 us (1%)
    pallas_call x4, Pallas kernels, attention(): pl.pallas_call(body, grid=steps, in_specs=[pl.BlockSpec((1, 128, bq), lam...  154 us
    pallas_call x2, Pallas kernels, tail(): pl.pallas_call(body, grid=(1,), in_specs=[pl.BlockSpec(memory_space=pltpu...  125 us
    pallas_call x2, Pallas kernels, qkv(): pl.pallas_call(body, grid=(TP,), in_specs=[pl.BlockSpec(mods.shape, lambd...  99.8 us
    pallas_call x1, Pallas kernels, finish(): pl.pallas_call(body, in_specs=[vm] * 3, out_specs=vm, out_shape=jax.Shape...  10.3 us

profile of v1, /device:TPU:0, one launch (start us, length us, event | category | flops | bytes accessed | tf_op | source)
XLA Modules:
  0.0 403.6 jit_solution(6942365731790071397)
XLA Ops:
  0.0 0.0 copy-start
  0.8 1.0 copy-done
  1.8 0.8 reduce
  2.6 1.3 broadcast_in_dim.2.refs_7_
  4.0 0.8 copy.25
  4.7 1.4 convert_add_fusion.refs_0_.refs_1_
  6.2 1.9 fusion
  8.1 0.9 copy.26
  8.9 31.3 %qkv_1.1 = (bf16[4,128,4096]{2,1,0:T(8,128)(2,1)}, bf16[4096,512]{1,0:T(8,128)(2,1)}, bf16[4,72,4096]{2,1,0:T(8,128)(2,1)}, f32[4,16,128]{2,1,0:T(8,128)}, bf16[...) custom-call(f32[14,1152]{1,0:T(8,128)} %convert_add_fusion.refs_0_.r, ...), custom_call_target="tpu_custom_call" | custom-call | tf_op jit(solution)/shard_map/qkv_1/pallas_call | solution.py:232
  40.3 40.1 %attn_2.1 = (bf16[2,4,72,1024]{3,2,1,0:T(8,128)(2,1)}, bf16[1152,1152]{1,0:T(8,128)(2,1)}, bf16[288,1152]{1,0:T(8,128)(2,1)}, bf16[288,1152]{1,0:T(8,128)(2,1)},...) custom-call(bf16[4,128,4096]{2,1,0:T(8,128)(2,1)} %get-tuple-element, ...), custom_call_target="tpu_custom_call" | custom-call | tf_op jit(solution)/shard_map/attn_2/pallas_call | solution.py:304
  80.4 1.4 repair.4
  81.8 44.8 %attn_3.1 = (bf16[2,4,72,1024]{3,2,1,0:T(8,128)(2,1)}, bf16[288,1024]{1,0:T(8,128)(2,1)}, bf16[288,1024]{1,0:T(8,128)(2,1)}, bf16[576,1152]{1,0:T(8,128)(2,1)}, ...) custom-call(bf16[4,128,4096]{2,1,0:T(8,128)(2,1)} %get-tuple-element, ...), custom_call_target="tpu_custom_call" | custom-call | tf_op jit(solution)/shard_map/attn_3/pallas_call | solution.py:304
  126.6 0.9 repair.5
  127.6 65.3 %tail_4.1 = (f32[1024,1152]{1,0:T(8,128)}, bf16[1024,1152]{1,0:T(8,128)(2,1)}, bf16[576,1152]{1,0:T(8,128)(2,1)}, bf16[576,1152]{1,0:T(8,128)(2,1)}, bf16[576,11...) custom-call(s32[1]{0:T(128)S(6)} %copy.32.refs_0_, ...), custom_call_target="tpu_custom_call" | custom-call | tf_op jit(solution)/shard_map/tail_4/pallas_call | solution.py:563
  192.9 68.5 %qkv_5.1 = (bf16[4,128,4096]{2,1,0:T(8,128)(2,1)}, bf16[4096,512]{1,0:T(8,128)(2,1)}, bf16[4,72,4096]{2,1,0:T(8,128)(2,1)}, f32[4,16,128]{2,1,0:T(8,128)}, bf16[...) custom-call(f32[14,1152]{1,0:T(8,128)} %convert_add_fusion.refs_0_.r, ...), custom_call_target="tpu_custom_call" | custom-call | tf_op jit(solution)/shard_map/qkv_5/pallas_call | solution.py:232
  261.4 34.9 %attn_6.1 = (bf16[2,4,72,1024]{3,2,1,0:T(8,128)(2,1)}, bf16[576,1152]{1,0:T(8,128)(2,1)}, bf16[576,1152]{1,0:T(8,128)(2,1)}, bf16[288,1152]{1,0:T(8,128)(2,1)}, ...) custom-call(bf16[4,128,4096]{2,1,0:T(8,128)(2,1)} %get-tuple-element, ...), custom_call_target="tpu_custom_call" | custom-call | tf_op jit(solution)/shard_map/attn_6/pallas_call | solution.py:304
  296.3 0.9 repair.6
  297.2 33.8 %attn_7.1 = (bf16[2,4,72,1024]{3,2,1,0:T(8,128)(2,1)}, bf16[288,1024]{1,0:T(8,128)(2,1)}, bf16[288,1024]{1,0:T(8,128)(2,1)}, bf16[576,1152]{1,0:T(8,128)(2,1)}, ...) custom-call(bf16[4,128,4096]{2,1,0:T(8,128)(2,1)} %get-tuple-element, ...), custom_call_target="tpu_custom_call" | custom-call | tf_op jit(solution)/shard_map/attn_7/pallas_call | solution.py:304
  331.1 0.9 repair.7
  332.0 0.0 copy-start.1
  332.0 59.4 %tail_8.1 = (f32[32,1024]{1,0:T(8,128)}, bf16[576,1152]{1,0:T(8,128)(2,1)}, bf16[576,1152]{1,0:T(8,128)(2,1)}) custom-call(s32[1]{0:T(128)S(6)} %copy.32.refs_0_, f32[14,1152]{1,0:T(8,128)} %convert_add_fusion.refs_0_.refs_1_, bf16[2,8,72,128]{3,2,1,0:T(8,128)(2,1)} %bitcast.59, bf16[2,8,72,128]{3,2,1,0:T(8,128)(2,1)} %get-tuple-element.77.refs_3_, ...), custom_call_target="tpu_custom_call" | custom-call | tf_op jit(solution)/shard_map/tail_8/pallas_call | solution.py:563
  391.4 10.3 %finish.1 = f32[512,128]{1,0:T(8,128)} custom-call(f32[32,1024]{1,0:T(8,128)} %get-tuple-element.148.tok_ref, f32[512,128]{1,0:T(8,128)} %bitcast.66, f32[1,2]{1,0:T(1,128)} %ab_ref.1), custom_call_target="tpu_custom_call" | custom-call | tf_op jit(solution)/shard_map/finish/pallas_call | solution.py:628
  401.7 1.7 copy.33
  403.3 0.0 copy-done.1
  (2 shorter events, 0.1 us)
Async XLA Ops:
  0.0 1.8 copy-start
  332.0 71.4 %copy-start.1 = (bf16[2,1152,2,4,72]{1,4,3,2,0:T(8,128)(2,1)S(1)}, bf16[2,1152,2,4,72]{1,4,3,2,0:T(8,128)(2,1)}, u32[]{:S(2)}) copy-start(bf16[2,1152,2,4,72]{1,4,3,2,0:T(8,128)(2,1)} %param.29) | copy-start | bytes 7962628
